TPU v7x, 32 devices: a whole 2x2x4 slice. The times are simulated.
32 devices in a mesh: groups: 2 (over y), ctx: 4 (over x, core), head: 4 (over z).
Axes of the slice: x: 2, y: 2, z: 4, core: 2. Of those that a mesh axis runs over, the one named last changes fastest.
Arguments:
- queries: bfloat16 [384, 64, 128], P(('groups', 'ctx'), 'head'), parts along dimension 0, may hold values from -16 to 16
- prefix_keys: bfloat16 [16384, 8, 128], P(('groups', 'ctx'), 'head'), parts along dimension 0, may hold values from -16 to 16
- prefix_values: bfloat16 [16384, 8, 128], P(('groups', 'ctx'), 'head'), parts along dimension 0, may hold values from -12 to 12
- suffix_keys: bfloat16 [384, 512, 8, 128], P(('groups', 'ctx'), None, 'head'), parts along dimension 0, may hold values from -16 to 16
- suffix_values: bfloat16 [384, 512, 8, 128], P(('groups', 'ctx'), None, 'head'), parts along dimension 0, may hold values from -12 to 12
- lengths: int32 [384], P(('groups', 'ctx')), parts along dimension 0, may hold values from 1 to 512, as said below
Outputs:
- attended: bfloat16 [384, 64, 128], P(('groups', 'ctx'), 'head'), parts along dimension 0
There are 2 independent parts, one for each index of `groups`. A program takes and returns all parts, laid end to end along the dimension named above; each array names one. Nothing has to cross between parts.
Inputs may be any that keep to these rules, and one draw needn't show every extreme that they name: The live slots of a row are its first lengths[r] slots; some row of each part has exactly 512.
All inputs are finite; a program needn't handle non-finite values.
Results may differ from a plain program's by a relative error of at most 0.0025.
Values may be sent and summed in bfloat16 or wider, within the bound.
A program may use at most 128 MiB of HBM per device.

v0:
```python
import functools
import math

import jax
import jax.numpy as jnp
from jax import lax
from jax.experimental import pallas as pl
from jax.experimental.pallas import tpu as pltpu
from jax.sharding import PartitionSpec as P

F32 = jnp.float32
BF16 = jnp.bfloat16
MASKED = -1e30
LANES = 128


def dot_t(a, b):
    return lax.dot_general(a, b, (((1,), (1,)), ((), ())), preferred_element_type=F32)


def kernel(
    n_ctx, tile_rows, first_tiles,
    len_ref, q_hbm, pk_hbm, pv_hbm, sk_hbm, sv_hbm, out_ref,
    q_raw, qk, k_raw, v_raw, k_cut, v_cut, wide, sk, sv,
    part_acc, part_stat, got_acc, got_stat,
    own_acc, own_top, own_sum, suf_acc, suf_top, suf_sum,
    q_sem, kv_sem, suf_sem, q_send, q_recv, kv_send, kv_recv, p_send, p_recv,
):
    rows, heads, width = q_hbm.shape
    kv = k_cut.shape[1]
    group = heads // kv
    flat = rows * group
    pair = 2 if n_ctx % 2 == 0 else 1
    chips = n_ctx // pair
    blocks = pair
    factor = width ** (-0.5) * math.log2(math.e)
    tiles = rows // tile_rows
    slots = sk.shape[1]
    me = lax.axis_index("ctx")
    chip, core = me // pair, me % pair

    def device(chip_at, core_at):
        return {"ctx": chip_at * pair + core_at}

    def remote(src, dst, send, recv, target):
        return pltpu.make_async_remote_copy(
            src_ref=src, dst_ref=dst, send_sem=send, recv_sem=recv,
            device_id=target, device_id_type=pl.DeviceIdType.MESH,
        )

    q_copy = pltpu.make_async_copy(q_hbm, q_raw.at[0], q_sem)
    q_copy.start()
    kv_copies = [
        pltpu.make_async_copy(pk_hbm, k_raw.at[0], kv_sem.at[0]),
        pltpu.make_async_copy(pv_hbm, v_raw.at[0], kv_sem.at[1]),
    ]
    for copy in kv_copies:
        copy.start()

    def suffix_copies(tile):
        span = pl.ds(tile * tile_rows, tile_rows)
        return (
            pltpu.make_async_copy(sk_hbm.at[span], sk.at[span], suf_sem.at[tile, 0]),
            pltpu.make_async_copy(sv_hbm.at[span], sv.at[span], suf_sem.at[tile, 1]),
        )

    partners = [device(lax.rem(chip + t, chips), core) for t in range(1, chips)]
    backs = [device(lax.rem(chip - t + chips, chips), core) for t in range(1, chips)]
    twin = device(chip, pair - 1 - core)
    greeted = partners + ([twin] if pair == 2 else [])
    if greeted:
        barrier = pltpu.get_barrier_semaphore()
        for target in greeted:
            pl.semaphore_signal(
                barrier, inc=1, device_id=target, device_id_type=pl.DeviceIdType.MESH
            )
        pl.semaphore_wait(barrier, len(greeted))

    q_sends = [
        remote(q_hbm, q_raw.at[t + 1], q_send.at[t], q_recv.at[t], partners[t])
        for t in range(chips - 1)
    ]
    for copy in q_sends:
        copy.start()
    kv_sends = []
    if pair == 2:
        kv_sends = [
            remote(pk_hbm, k_raw.at[1], kv_send.at[0], kv_recv.at[0], twin),
            remote(pv_hbm, v_raw.at[1], kv_send.at[1], kv_recv.at[1], twin),
        ]
        for copy in kv_sends:
            copy.start()

    def start_tile(tile, carry):
        for copy in suffix_copies(tile):
            copy.start()
        return carry

    lax.fori_loop(0, tiles, start_tile, 0)

    def split_queries(slot):
        wide_q = q_raw[slot].astype(F32).reshape(rows, kv, group, width)
        for k in range(kv):
            qk[slot, k] = wide_q[:, k].reshape(flat, width).astype(BF16)

    span = k_cut.shape[2]
    piece = wide.shape[1]
    pieces = span * kv // piece

    def split_block(block):
        def step(i, carry):
            at = pl.ds(pl.multiple_of(i * piece, piece), piece)
            to = pl.ds(pl.multiple_of(i * (piece // kv), piece // kv), piece // kv)
            wide[0] = k_raw[block, at, :].astype(F32)
            wide[1] = v_raw[block, at, :].astype(F32)
            for k in range(kv):
                rows_k = pl.ds(k, piece // kv, stride=kv) if kv > 1 else pl.ds(0, piece)
                k_cut[block, k, to, :] = wide[0, rows_k, :].astype(BF16)
                v_cut[block, k, to, 0:width] = wide[1, rows_k, :].astype(BF16)
                v_cut[block, k, to, width : 2 * width] = jnp.ones((piece // kv, width), BF16)
            return carry

        lax.fori_loop(0, pieces, step, 0)

    step_rows = LANES

    def block_terms(slot, k, block, at):
        scores = dot_t(qk[slot, k, at, :], k_cut[block, k]) * factor
        top = jnp.max(scores, axis=1, keepdims=True)
        weights = jnp.exp2(scores - top).astype(BF16)
        both = jnp.dot(weights, v_cut[block, k], preferred_element_type=F32)
        return top, both[:, :width], both[:, width:]

    def merge(one, two):
        top = jnp.maximum(one[0], two[0])
        a, b = jnp.exp2(one[0] - top), jnp.exp2(two[0] - top)
        return top, one[1] * a + two[1] * b, one[2] * a + two[2] * b

    chunks = flat // step_rows

    def own_block(block):
        def step(k, carry):
            for c in range(chunks):
                at = pl.ds(c * step_rows, step_rows)
                terms = block_terms(0, k, block, at)
                if block > 0:
                    terms = merge(terms, (own_top[k, at, :], own_acc[k, at, :], own_sum[k, at, :]))
                own_top[k, at, :] = jnp.broadcast_to(terms[0], (step_rows, width))
                own_acc[k, at, :] = terms[1]
                own_sum[k, at, :] = terms[2]
            return carry

        lax.fori_loop(0, kv, step, 0)

    diagonal = lax.broadcasted_iota(jnp.int32, (step_rows, LANES), 0) == lax.broadcasted_iota(
        jnp.int32, (step_rows, LANES), 1
    )

    def partial_copies(t, k):
        return (
            remote(part_acc.at[t, k], got_acc.at[t, k], p_send.at[t, k, 0], p_recv.at[t, k, 0], backs[t]),
            remote(part_stat.at[t, k], got_stat.at[t, k], p_send.at[t, k, 1], p_recv.at[t, k, 1], backs[t]),
        )

    def remote_rows(t):
        for k in range(kv):
            stat = []
            for c in range(chunks):
                at = pl.ds(c * step_rows, step_rows)
                terms = block_terms(t + 1, k, 0, at)
                for block in range(1, blocks):
                    terms = merge(terms, block_terms(t + 1, k, block, at))
                part_acc[t, k, at, :] = terms[1]
                top_wide = jnp.broadcast_to(terms[0], (step_rows, LANES))
                for i, x in enumerate((top_wide, terms[2])):
                    row = 2 * c + i
                    part_stat[t, k, row : row + 1, :] = jnp.sum(
                        jnp.where(diagonal, x, 0.0), axis=0, keepdims=True
                    )
            for copy in partial_copies(t, k):
                copy.start()

    column = lax.broadcasted_iota(jnp.int32, (heads, slots), 1)
    same_head = column % kv == lax.broadcasted_iota(jnp.int32, (heads, slots), 0) // group

    def suffix_tile(tile, carry):
        for copy in suffix_copies(tile):
            copy.wait()
        for i in range(tile_rows):
            r = tile * tile_rows + i
            live = same_head & (column < len_ref[r] * kv)
            scores = jnp.where(live, dot_t(q_raw[0, r], sk[r]) * factor, MASKED)
            top = jnp.max(scores, axis=1, keepdims=True)
            weights = jnp.exp2(scores - top).astype(BF16)
            total = jnp.sum(weights.astype(F32), axis=1, keepdims=True)
            acc = jnp.dot(weights, sv[r], preferred_element_type=F32)
            top = jnp.broadcast_to(top, (heads, width))
            total = jnp.broadcast_to(total, (heads, width))
            to = pl.ds(pl.multiple_of(r * group, group), group)
            for k in range(kv):
                part = slice(k * group, (k + 1) * group)
                suf_acc[k, to, :] = acc[part]
                suf_top[k, to, :] = top[part]
                suf_sum[k, to, :] = total[part]
        return carry

    q_copy.wait()
    split_queries(0)
    for copy in kv_copies:
        copy.wait()
    split_block(0)
    own_block(0)
    lax.fori_loop(0, first_tiles, suffix_tile, 0)
    for copy in kv_sends:
        copy.wait_recv()
    for block in range(1, blocks):
        split_block(block)
    for t in range(chips - 1):
        q_sends[t].wait_recv()
        split_queries(t + 1)
        remote_rows(t)
    for block in range(1, blocks):
        own_block(block)
    lax.fori_loop(first_tiles, tiles, suffix_tile, 0)

    for k in range(kv):
        for t in range(chips - 1):
            for copy in partial_copies(t, k):
                copy.wait_recv()
    per = step_rows // group
    for c in range(chunks):
        at = pl.ds(c * step_rows, step_rows)
        done = []
        for k in range(kv):
            terms = merge(
                (own_top[k, at, :], own_acc[k, at, :], own_sum[k, at, :]),
                (suf_top[k, at, :], suf_acc[k, at, :], suf_sum[k, at, :]),
            )
            for t in range(chips - 1):
                stats = []
                for i in range(2):
                    row = jnp.broadcast_to(
                        got_stat[t, k, 2 * c + i : 2 * c + i + 1, :], (step_rows, LANES)
                    )
                    stats.append(jnp.sum(jnp.where(diagonal, row, 0.0), axis=1, keepdims=True))
                terms = merge(terms, (stats[0], got_acc[t, k, at, :], stats[1]))
            done.append((terms[1] / terms[2]).reshape(per, 1, group, width))
        joined = jnp.concatenate(done, axis=1).reshape(per, heads, width)
        out_ref[c * per : (c + 1) * per] = joined.astype(BF16)
    for copy in q_sends + kv_sends:
        copy.wait_send()
    for t in range(chips - 1):
        for k in range(kv):
            for copy in partial_copies(t, k):
                copy.wait_send()


def shards(n_ctx, queries, prefix_keys, prefix_values, suffix_keys, suffix_values, lengths):
    rows, heads, width = queries.shape
    positions, kv, _ = prefix_keys.shape
    slots = suffix_keys.shape[1] * kv
    flat = rows * (heads // kv)
    pair = 2 if n_ctx % 2 == 0 else 1
    others = max(1, n_ctx // pair - 1)
    tile_rows = math.gcd(rows, 4)
    tiles = rows // tile_rows
    first_tiles = tiles // 3
    stat_rows = -(-2 * (flat // LANES) // 8) * 8
    piece = math.gcd(positions * kv, 1024)
    anywhere = pl.BlockSpec(memory_space=pl.ANY)
    vmem = pltpu.VMEM
    dma = pltpu.SemaphoreType.DMA
    call = pl.pallas_call(
        functools.partial(kernel, n_ctx, tile_rows, first_tiles),
        out_shape=jax.ShapeDtypeStruct((rows, heads, width), BF16),
        in_specs=[pl.BlockSpec(memory_space=pltpu.SMEM)] + [anywhere] * 5,
        out_specs=pl.BlockSpec(memory_space=vmem),
        scratch_shapes=[
            vmem((1 + others, rows, heads, width), BF16),
            vmem((1 + others, kv, flat, width), BF16),
            vmem((pair, positions * kv, width), BF16),
            vmem((pair, positions * kv, width), BF16),
            vmem((pair, kv, positions, width), BF16),
            vmem((pair, kv, positions, 2 * width), BF16),
            vmem((2, piece, width), F32),
            vmem((rows, slots, width), BF16),
            vmem((rows, slots, width), BF16),
            vmem((others, kv, flat, width), F32),
            vmem((others, kv, stat_rows, LANES), F32),
            vmem((others, kv, flat, width), F32),
            vmem((others, kv, stat_rows, LANES), F32),
        ]
        + [vmem((kv, flat, width), F32)] * 6
        + [
            dma,
            dma((2,)),
            dma((tiles, 2)),
            dma((others,)),
            dma((others,)),
            dma((2,)),
            dma((2,)),
            dma((others, kv, 2)),
            dma((others, kv, 2)),
        ],
        compiler_params=pltpu.CompilerParams(
            collective_id=0, has_side_effects=True, vmem_limit_bytes=62 * 1024 * 1024
        ),
    )
    return call(
        lengths,
        queries,
        prefix_keys.reshape(positions * kv, width),
        prefix_values.reshape(positions * kv, width),
        suffix_keys.reshape(rows, slots, width),
        suffix_values.reshape(rows, slots, width),
    )


def solution(mesh):
    placed = (
        P(("groups", "ctx"), "head", None),
        P(("groups", "ctx"), "head", None),
        P(("groups", "ctx"), "head", None),
        P(("groups", "ctx"), None, "head", None),
        P(("groups", "ctx"), None, "head", None),
        P(("groups", "ctx")),
    )
    return jax.shard_map(
        functools.partial(shards, mesh.shape["ctx"]),
        mesh=mesh,
        in_specs=placed,
        out_specs=P(("groups", "ctx"), "head", None),
        check_vma=False,
    )
```

profile of v0, /device:TPU:0, one launch (start us, length us, event | category | flops | bytes accessed | tf_op | source)
XLA Modules:
  0.0 34.7 jit_solution(14721228325990595025)
XLA Ops:
  0.0 33.0 %shard_map.64 = bf16[48,16,128]{2,1,0:T(8,128)(2,1)} custom-call(s32[48]{0:T(128)} %len_ref.1, bf16[48,16,128]{2,1,0:T(8,128)(2,1)} %q_hbm.1, bf16[4096,128]{1,0:T(8,128)(2,1)} %bitcast.6, bf16[4096,128]{1,0:T(8,128)(2,1)} %bitcast.7, bf16[48,1024,128]{2,1,0:T(8,128)(2,1)} %bitcast.4, bf16[48,1024,128]{2,1,0:T(8,128)(2,1)} %bitcast.5), custom_call_target="tpu_custom_call" | custom-call | tf_op jit(solution)/shard_map/pallas_call | solution.py:309
  33.0 1.6 %copy.8 = bf16[48,16,128]{2,1,0:T(8,128)(2,1)} copy(bf16[48,16,128]{2,1,0:T(8,128)(2,1)} %shard_map.64) | data formatting | bytes 393216
where the time goes:
time: 34.8 us; the launch traced here: 34.7 us
  Pallas kernels  33 us (95%)
  local copies, waits for them, and re-layouts  1.62 us (5%)
    pallas_call x1, Pallas kernels, shards(): call(lengths, queries, prefix_keys.reshape(positions * kv, width), prefix...  33 us
    unnamed x1, local copies, waits for them, and re-layouts  1.62 us

commit v1 on v0

--- a/solution.py
+++ b/solution.py
@@ -123,31 +123,28 @@
         lax.fori_loop(0, pieces, step, 0)
 
     step_rows = LANES
-
-    def block_terms(slot, k, block, at):
-        scores = dot_t(qk[slot, k, at, :], k_cut[block, k]) * factor
+    chunks = flat // step_rows
+
+    def block_terms(slot, k, block):
+        scores = dot_t(qk[slot, k], k_cut[block, k])
         top = jnp.max(scores, axis=1, keepdims=True)
-        weights = jnp.exp2(scores - top).astype(BF16)
+        weights = jnp.exp2((scores - top) * factor).astype(BF16)
         both = jnp.dot(weights, v_cut[block, k], preferred_element_type=F32)
-        return top, both[:, :width], both[:, width:]
+        return top * factor, both[:, :width], both[:, width:]
 
     def merge(one, two):
         top = jnp.maximum(one[0], two[0])
         a, b = jnp.exp2(one[0] - top), jnp.exp2(two[0] - top)
         return top, one[1] * a + two[1] * b, one[2] * a + two[2] * b
 
-    chunks = flat // step_rows
-
     def own_block(block):
         def step(k, carry):
-            for c in range(chunks):
-                at = pl.ds(c * step_rows, step_rows)
-                terms = block_terms(0, k, block, at)
-                if block > 0:
-                    terms = merge(terms, (own_top[k, at, :], own_acc[k, at, :], own_sum[k, at, :]))
-                own_top[k, at, :] = jnp.broadcast_to(terms[0], (step_rows, width))
-                own_acc[k, at, :] = terms[1]
-                own_sum[k, at, :] = terms[2]
+            terms = block_terms(0, k, block)
+            if block > 0:
+                terms = merge(terms, (own_top[k], own_acc[k], own_sum[k]))
+            own_top[k] = jnp.broadcast_to(terms[0], (flat, width))
+            own_acc[k] = terms[1]
+            own_sum[k] = terms[2]
             return carry
 
         lax.fori_loop(0, kv, step, 0)
@@ -164,44 +161,62 @@
 
     def remote_rows(t):
         for k in range(kv):
-            stat = []
+            terms = block_terms(t + 1, k, 0)
+            for block in range(1, blocks):
+                terms = merge(terms, block_terms(t + 1, k, block))
+            part_acc[t, k] = terms[1]
+            top_wide = jnp.broadcast_to(terms[0], (flat, LANES))
             for c in range(chunks):
-                at = pl.ds(c * step_rows, step_rows)
-                terms = block_terms(t + 1, k, 0, at)
-                for block in range(1, blocks):
-                    terms = merge(terms, block_terms(t + 1, k, block, at))
-                part_acc[t, k, at, :] = terms[1]
-                top_wide = jnp.broadcast_to(terms[0], (step_rows, LANES))
+                at = slice(c * step_rows, (c + 1) * step_rows)
                 for i, x in enumerate((top_wide, terms[2])):
                     row = 2 * c + i
                     part_stat[t, k, row : row + 1, :] = jnp.sum(
-                        jnp.where(diagonal, x, 0.0), axis=0, keepdims=True
+                        jnp.where(diagonal, x[at], 0.0), axis=0, keepdims=True
                     )
             for copy in partial_copies(t, k):
                 copy.start()
 
     column = lax.broadcasted_iota(jnp.int32, (heads, slots), 1)
     same_head = column % kv == lax.broadcasted_iota(jnp.int32, (heads, slots), 0) // group
-
-    def suffix_tile(tile, carry):
-        for copy in suffix_copies(tile):
-            copy.wait()
-        for i in range(tile_rows):
-            r = tile * tile_rows + i
-            live = same_head & (column < len_ref[r] * kv)
-            scores = jnp.where(live, dot_t(q_raw[0, r], sk[r]) * factor, MASKED)
+    nothing = jnp.zeros((heads, width), BF16)
+
+    def suffix_pair(r):
+        ask = jnp.concatenate(
+            [
+                jnp.concatenate([q_raw[0, r], nothing], axis=1),
+                jnp.concatenate([nothing, q_raw[0, r + 1]], axis=1),
+            ],
+            axis=0,
+        )
+        both = dot_t(ask, jnp.concatenate([sk[r], sk[r + 1]], axis=1))
+        done = []
+        for i in range(2):
+            live = same_head & (column < len_ref[r + i] * kv)
+            scores = jnp.where(live, both[i * heads : (i + 1) * heads], MASKED)
             top = jnp.max(scores, axis=1, keepdims=True)
-            weights = jnp.exp2(scores - top).astype(BF16)
+            weights = jnp.exp2((scores - top) * factor).astype(BF16)
             total = jnp.sum(weights.astype(F32), axis=1, keepdims=True)
-            acc = jnp.dot(weights, sv[r], preferred_element_type=F32)
-            top = jnp.broadcast_to(top, (heads, width))
-            total = jnp.broadcast_to(total, (heads, width))
-            to = pl.ds(pl.multiple_of(r * group, group), group)
+            done.append((top * factor, weights, total))
+        joined = jnp.concatenate([x[1] for x in done], axis=0)
+        out = jnp.dot(
+            joined, jnp.concatenate([sv[r], sv[r + 1]], axis=1), preferred_element_type=F32
+        )
+        for i in range(2):
+            acc = out[i * heads : (i + 1) * heads, i * width : (i + 1) * width]
+            top = jnp.broadcast_to(done[i][0], (heads, width))
+            total = jnp.broadcast_to(done[i][2], (heads, width))
+            to = pl.ds(pl.multiple_of((r + i) * group, group), group)
             for k in range(kv):
                 part = slice(k * group, (k + 1) * group)
                 suf_acc[k, to, :] = acc[part]
                 suf_top[k, to, :] = top[part]
                 suf_sum[k, to, :] = total[part]
+
+    def suffix_tile(tile, carry):
+        for copy in suffix_copies(tile):
+            copy.wait()
+        for i in range(0, tile_rows, 2):
+            suffix_pair(tile * tile_rows + i)
         return carry
 
     q_copy.wait()
@@ -262,7 +277,7 @@
     flat = rows * (heads // kv)
     pair = 2 if n_ctx % 2 == 0 else 1
     others = max(1, n_ctx // pair - 1)
-    tile_rows = math.gcd(rows, 4)
+    tile_rows = math.gcd(rows, 8)
     tiles = rows // tile_rows
     first_tiles = tiles // 3
     stat_rows = -(-2 * (flat // LANES) // 8) * 8

time: 34.8 us -> 32.1 us (0.922)
  Pallas kernels: 33 us -> 30.3 us
    pallas_call x1, Pallas kernels: 33 us -> 30.3 us  [shards(): call(lengths, queries, prefix_keys.reshape(positions * kv, width), prefix...]
where the time goes in v1:
time: 32.1 us; the launch traced here: 32 us
  Pallas kernels  30.3 us (94%)
  local copies, waits for them, and re-layouts  1.62 us (5%)
    pallas_call x1, Pallas kernels, shards(): call(lengths, queries, prefix_keys.reshape(positions * kv, width), prefix...  30.3 us
    unnamed x1, local copies, waits for them, and re-layouts  1.62 us

profile of v1, /device:TPU:0, one launch (start us, length us, event | category | flops | bytes accessed | tf_op | source)
XLA Modules:
  0.0 32.0 jit_solution(9325295879983054722)
XLA Ops:
  0.0 30.3 %shard_map.64 = bf16[48,16,128]{2,1,0:T(8,128)(2,1)} custom-call(s32[48]{0:T(128)} %len_ref.1, bf16[48,16,128]{2,1,0:T(8,128)(2,1)} %q_hbm.1, bf16[4096,128]{1,0:T(8,128)(2,1)} %bitcast.6, bf16[4096,128]{1,0:T(8,128)(2,1)} %bitcast.7, bf16[48,1024,128]{2,1,0:T(8,128)(2,1)} %bitcast.4, bf16[48,1024,128]{2,1,0:T(8,128)(2,1)} %bitcast.5), custom_call_target="tpu_custom_call" | custom-call | tf_op jit(solution)/shard_map/pallas_call | solution.py:324
  30.3 1.6 %copy.8 = bf16[48,16,128]{2,1,0:T(8,128)(2,1)} copy(bf16[48,16,128]{2,1,0:T(8,128)(2,1)} %shard_map.64) | data formatting | bytes 393216

commit v2 on v1

v2 whole, which is shorter than its diff:
```python
import functools
import math

import jax
import jax.numpy as jnp
from jax import lax
from jax.experimental import pallas as pl
from jax.experimental.pallas import tpu as pltpu
from jax.sharding import PartitionSpec as P

F32 = jnp.float32
BF16 = jnp.bfloat16
MASKED = -1e30
LANES = 128


def dot_t(a, b):
    return lax.dot_general(a, b, (((1,), (1,)), ((), ())), preferred_element_type=F32)


def kernel(
    n_ctx, tile_rows, first_tiles,
    len_ref, q_hbm, pk_hbm, pv_hbm, sk_hbm, sv_hbm, out_ref,
    q_raw, qk, k_raw, v_raw, k_cut, v_turn, wide, sk, sv,
    scores_a, scores_b, weights_a, weights_b, top_a, top_b,
    acc_all, top_all, part, got, suf_acc, suf_top, suf_sum,
    q_sem, kv_sem, suf_sem, q_send, q_recv, kv_send, kv_recv, p_send, p_recv,
):
    rows, heads, width = q_hbm.shape
    kv = k_cut.shape[1]
    group = heads // kv
    flat = rows * group
    pair = 2 if n_ctx % 2 == 0 else 1
    chips = n_ctx // pair
    blocks = pair
    factor = width ** (-0.5) * math.log2(math.e)
    tiles = rows // tile_rows
    slots = sk.shape[1]
    span = k_cut.shape[2]
    tall = v_turn.shape[2]
    columns = scores_a.shape[1]
    me = lax.axis_index("ctx")
    chip, core = me // pair, me % pair

    def device(chip_at, core_at):
        return {"ctx": chip_at * pair + core_at}

    def remote(src, dst, send, recv, target):
        return pltpu.make_async_remote_copy(
            src_ref=src, dst_ref=dst, send_sem=send, recv_sem=recv,
            device_id=target, device_id_type=pl.DeviceIdType.MESH,
        )

    q_copy = pltpu.make_async_copy(q_hbm, q_raw.at[0], q_sem)
    q_copy.start()
    kv_copies = [
        pltpu.make_async_copy(pk_hbm, k_raw, kv_sem.at[0]),
        pltpu.make_async_copy(pv_hbm, v_raw, kv_sem.at[1]),
    ]
    for copy in kv_copies:
        copy.start()

    def suffix_copies(tile):
        at = pl.ds(tile * tile_rows, tile_rows)
        return (
            pltpu.make_async_copy(sk_hbm.at[at], sk.at[at], suf_sem.at[tile, 0]),
            pltpu.make_async_copy(sv_hbm.at[at], sv.at[at], suf_sem.at[tile, 1]),
        )

    partners = [device(lax.rem(chip + t, chips), core) for t in range(1, chips)]
    backs = [device(lax.rem(chip - t + chips, chips), core) for t in range(1, chips)]
    twin = device(chip, pair - 1 - core)
    greeted = partners + ([twin] if pair == 2 else [])
    if greeted:
        barrier = pltpu.get_barrier_semaphore()
        for target in greeted:
            pl.semaphore_signal(
                barrier, inc=1, device_id=target, device_id_type=pl.DeviceIdType.MESH
            )
        pl.semaphore_wait(barrier, len(greeted))

    q_sends = [
        remote(q_hbm, q_raw.at[t + 1], q_send.at[t], q_recv.at[t], partners[t])
        for t in range(chips - 1)
    ]
    for copy in q_sends:
        copy.start()

    def start_tile(tile, carry):
        for copy in suffix_copies(tile):
            copy.start()
        return carry

    lax.fori_loop(0, tiles, start_tile, 0)

    def split_queries(slot):
        wide_q = q_raw[slot].astype(F32).reshape(rows, kv, group, width)
        for k in range(kv):
            qk[k, slot * flat : (slot + 1) * flat] = wide_q[:, k].reshape(flat, width).astype(BF16)

    piece = wide.shape[1]
    cut = piece // kv

    def rows_of(k):
        return pl.ds(k, cut, stride=kv) if kv > 1 else pl.ds(0, piece)

    def split_keys():
        def step(i, carry):
            wide[0] = k_raw[pl.ds(pl.multiple_of(i * piece, piece), piece), :].astype(F32)
            to = pl.ds(pl.multiple_of(i * cut, cut), cut)
            for k in range(kv):
                k_cut[0, k, to, :] = wide[0, rows_of(k), :].astype(BF16)
            return carry

        lax.fori_loop(0, span * kv // piece, step, 0)

    def turn_values():
        ones = (lax.broadcasted_iota(jnp.int32, (tall - width, span), 0) == 0).astype(F32)
        for k in range(kv):
            v_turn[0, k, width:tall, :] = ones.astype(BF16)
        for i in range(span * kv // piece):
            wide[1] = v_raw[i * piece : (i + 1) * piece, :].astype(F32)
            for k in range(kv):
                turned = jnp.transpose(wide[1, rows_of(k), :])
                v_turn[0, k, 0:width, i * cut : (i + 1) * cut] = turned.astype(BF16)

    def kv_sends(k):
        if pair == 1:
            return []
        return [
            remote(k_cut.at[0, k], k_cut.at[1, k], kv_send.at[k, 0], kv_recv.at[k, 0], twin),
            remote(v_turn.at[0, k], v_turn.at[1, k], kv_send.at[k, 1], kv_recv.at[k, 1], twin),
        ]

    def merge(one, two):
        top = jnp.maximum(one[0], two[0])
        a, b = jnp.exp2(one[0] - top), jnp.exp2(two[0] - top)
        return top, one[1] * a + two[1] * b, one[2] * a + two[2] * b

    buffers = ((scores_a, weights_a, top_a), (scores_b, weights_b, top_b))
    height = math.gcd(span, 256)

    def unit_scores(unit, at):
        block, k, tile = unit
        scores, _, tops = buffers[at]
        ask = qk[k, tile * columns : (tile + 1) * columns]
        top = None
        for j in range(span // height):
            part_of = slice(j * height, (j + 1) * height)
            x = dot_t(k_cut[block, k, part_of], ask)
            scores[part_of] = x
            x = jnp.max(x.reshape(height // 8, 8, columns), axis=0)
            top = x if top is None else jnp.maximum(top, x)
        tops[...] = jnp.broadcast_to(jnp.max(top, axis=0, keepdims=True), (8, columns))

    def unit_sums(unit, at):
        block, k, tile = unit
        scores, weights, tops = buffers[at]
        for j in range(span // height):
            part_of = slice(j * height, (j + 1) * height)
            x = scores[part_of].reshape(height // 8, 8, columns)
            x = jnp.exp2((x - tops[...][None]) * factor)
            weights[part_of] = x.reshape(height, columns).astype(BF16)
        out = jnp.dot(v_turn[block, k], weights[...], preferred_element_type=F32)
        top = tops[...] * factor
        to = slice(tile * columns, (tile + 1) * columns)
        if block > 0:
            old = top_all[k, :, to]
            new = jnp.maximum(old, top)
            a, b = jnp.exp2(old - new), jnp.exp2(top - new)
            out = acc_all[k, :, to] * a[0:1] + out * b[0:1]
            top = new
        if block < blocks - 1:
            acc_all[k, :, to] = out
            top_all[k, :, to] = top
            return
        first = lax.broadcasted_iota(jnp.int32, (8, LANES), 0) == 0
        for c in range(columns // LANES):
            at_c = tile * columns + c * LANES
            here = slice(c * LANES, (c + 1) * LANES)
            slot, within = at_c // flat, at_c % flat
            if slot == 0:
                acc_all[k, :, at_c : at_c + LANES] = out[:, here]
                top_all[k, :, at_c : at_c + LANES] = top[:, here]
            else:
                into = slice(within, within + LANES)
                part[slot - 1, k, 0:width, into] = out[0:width, here]
                part[slot - 1, k, width : width + 8, into] = jnp.where(
                    first, out[width : width + 8, here], top[:, here]
                )

    def partial_copy(t, k):
        return remote(part.at[t, k], got.at[t, k], p_send.at[t, k], p_recv.at[t, k], backs[t])

    def run_units(steps):
        steps = list(steps)
        for i, (before, unit, after) in enumerate(steps):
            if i == 0:
                before()
                unit_scores(unit, 0)
            if i + 1 < len(steps):
                steps[i + 1][0]()
                unit_scores(steps[i + 1][1], (i + 1) % 2)
            unit_sums(unit, i % 2)
            after()

    def nop():
        pass

    column = lax.broadcasted_iota(jnp.int32, (heads, slots), 1)
    same_head = column % kv == lax.broadcasted_iota(jnp.int32, (heads, slots), 0) // group
    nothing = jnp.zeros((heads, width), BF16)

    def suffix_pair(r):
        ask = jnp.concatenate(
            [
                jnp.concatenate([q_raw[0, r], nothing], axis=1),
                jnp.concatenate([nothing, q_raw[0, r + 1]], axis=1),
            ],
            axis=0,
        )
        both = dot_t(ask, jnp.concatenate([sk[r], sk[r + 1]], axis=1))
        done = []
        for i in range(2):
            live = same_head & (column < len_ref[r + i] * kv)
            scores = jnp.where(live, both[i * heads : (i + 1) * heads], MASKED)
            top = jnp.max(scores, axis=1, keepdims=True)
            weights = jnp.exp2((scores - top) * factor).astype(BF16)
            total = jnp.sum(weights.astype(F32), axis=1, keepdims=True)
            done.append((top * factor, weights, total))
        joined = jnp.concatenate([x[1] for x in done], axis=0)
        out = jnp.dot(
            joined, jnp.concatenate([sv[r], sv[r + 1]], axis=1), preferred_element_type=F32
        )
        for i in range(2):
            acc = out[i * heads : (i + 1) * heads, i * width : (i + 1) * width]
            top = jnp.broadcast_to(done[i][0], (heads, width))
            total = jnp.broadcast_to(done[i][2], (heads, width))
            to = pl.ds(pl.multiple_of((r + i) * group, group), group)
            for k in range(kv):
                part = slice(k * group, (k + 1) * group)
                suf_acc[k, to, :] = acc[part]
                suf_top[k, to, :] = top[part]
                suf_sum[k, to, :] = total[part]

    def suffix_tile(tile, carry):
        for copy in suffix_copies(tile):
            copy.wait()
        for i in range(0, tile_rows, 2):
            suffix_pair(tile * tile_rows + i)
        return carry

    all_tiles = chips * flat // columns
    near = flat // columns

    q_copy.wait()
    split_queries(0)
    kv_copies[0].wait()
    split_keys()
    kv_copies[1].wait()
    turn_values()
    for k in range(kv):
        for copy in kv_sends(k):
            copy.start()
    run_units([(nop, (0, k, tile), nop) for tile in range(near) for k in range(kv)])
    lax.fori_loop(0, first_tiles, suffix_tile, 0)

    waited = set()

    def ready(block, k, tile):
        def go():
            last = ((tile + 1) * columns - 1) // flat
            for t in range(last):
                if ("q", t) not in waited:
                    waited.add(("q", t))
                    q_sends[t].wait_recv()
                    split_queries(t + 1)
            if block > 0 and ("kv", k) not in waited:
                waited.add(("kv", k))
                for copy in kv_sends(k):
                    copy.wait_recv()

        return go

    def finish(block, k, tile):
        def go():
            if block == blocks - 1:
                for t in range(chips - 1):
                    end = (t + 2) * flat
                    if tile * columns < end <= (tile + 1) * columns:
                        partial_copy(t, k).start()

        return go

    order = [
        (block, k, tile) for k in range(kv) for tile in range(near, all_tiles) for block in range(blocks)
    ] + [(block, k, tile) for k in range(kv) for tile in range(near) for block in range(1, blocks)]
    run_units([(ready(*unit), unit, finish(*unit)) for unit in order])
    lax.fori_loop(first_tiles, tiles, suffix_tile, 0)

    for k in range(kv):
        for t in range(chips - 1):
            partial_copy(t, k).wait_recv()
    diagonal = lax.broadcasted_iota(jnp.int32, (LANES, LANES), 0) == lax.broadcasted_iota(
        jnp.int32, (LANES, LANES), 1
    )

    def upright(row):
        wide_row = jnp.broadcast_to(row, (LANES, LANES))
        return jnp.sum(jnp.where(diagonal, wide_row, 0.0), axis=1, keepdims=True)

    per = LANES // group
    for c in range(flat // LANES):
        at = slice(c * LANES, (c + 1) * LANES)
        done = []
        for k in range(kv):
            terms = (
                top_all[k, 0:1, at],
                acc_all[k, 0:width, at],
                acc_all[k, width : width + 1, at],
            )
            for t in range(chips - 1):
                terms = merge(
                    terms,
                    (
                        got[t, k, width + 1 : width + 2, at],
                        got[t, k, 0:width, at],
                        got[t, k, width : width + 1, at],
                    ),
                )
            terms = merge(
                (upright(terms[0]), jnp.transpose(terms[1]), upright(terms[2])),
                (suf_top[k, at, :], suf_acc[k, at, :], suf_sum[k, at, :]),
            )
            done.append((terms[1] / terms[2]).reshape(per, 1, group, width))
        joined = jnp.concatenate(done, axis=1).reshape(per, heads, width)
        out_ref[c * per : (c + 1) * per] = joined.astype(BF16)
    for copy in q_sends:
        copy.wait_send()
    for k in range(kv):
        for copy in kv_sends(k):
            copy.wait_send()
        for t in range(chips - 1):
            partial_copy(t, k).wait_send()


def shards(n_ctx, queries, prefix_keys, prefix_values, suffix_keys, suffix_values, lengths):
    rows, heads, width = queries.shape
    positions, kv, _ = prefix_keys.shape
    slots = suffix_keys.shape[1] * kv
    flat = rows * (heads // kv)
    pair = 2 if n_ctx % 2 == 0 else 1
    others = max(1, n_ctx // pair - 1)
    tile_rows = math.gcd(rows, 8)
    tiles = rows // tile_rows
    first_tiles = tiles // 3
    columns = math.gcd(n_ctx // pair * flat, 256)
    tall = width + 16
    piece = math.gcd(positions * kv, 1024)
    anywhere = pl.BlockSpec(memory_space=pl.ANY)
    vmem = pltpu.VMEM
    dma = pltpu.SemaphoreType.DMA
    call = pl.pallas_call(
        functools.partial(kernel, n_ctx, tile_rows, first_tiles),
        out_shape=jax.ShapeDtypeStruct((rows, heads, width), BF16),
        in_specs=[pl.BlockSpec(memory_space=pltpu.SMEM)] + [anywhere] * 5,
        out_specs=pl.BlockSpec(memory_space=vmem),
        scratch_shapes=[
            vmem((1 + others, rows, heads, width), BF16),
            vmem((kv, n_ctx // pair * flat, width), BF16),
            vmem((positions * kv, width), BF16),
            vmem((positions * kv, width), BF16),
            vmem((pair, kv, positions, width), BF16),
            vmem((pair, kv, tall, positions), BF16),
            vmem((2, piece, width), F32),
            vmem((rows, slots, width), BF16),
            vmem((rows, slots, width), BF16),
            vmem((positions, columns), F32),
            vmem((positions, columns), F32),
            vmem((positions, columns), BF16),
            vmem((positions, columns), BF16),
            vmem((8, columns), F32),
            vmem((8, columns), F32),
            vmem((kv, tall, n_ctx // pair * flat), F32),
            vmem((kv, 8, n_ctx // pair * flat), F32),
            vmem((others, kv, width + 8, flat), F32),
            vmem((others, kv, width + 8, flat), F32),
        ]
        + [vmem((kv, flat, width), F32)] * 3
        + [
            dma,
            dma((2,)),
            dma((tiles, 2)),
            dma((others,)),
            dma((others,)),
            dma((kv, 2)),
            dma((kv, 2)),
            dma((others, kv)),
            dma((others, kv)),
        ],
        compiler_params=pltpu.CompilerParams(
            collective_id=0, has_side_effects=True, vmem_limit_bytes=62 * 1024 * 1024
        ),
    )
    return call(
        lengths,
        queries,
        prefix_keys.reshape(positions * kv, width),
        prefix_values.reshape(positions * kv, width),
        suffix_keys.reshape(rows, slots, width),
        suffix_values.reshape(rows, slots, width),
    )


def solution(mesh):
    placed = (
        P(("groups", "ctx"), "head", None),
        P(("groups", "ctx"), "head", None),
        P(("groups", "ctx"), "head", None),
        P(("groups", "ctx"), None, "head", None),
        P(("groups", "ctx"), None, "head", None),
        P(("groups", "ctx")),
    )
    return jax.shard_map(
        functools.partial(shards, mesh.shape["ctx"]),
        mesh=mesh,
        in_specs=placed,
        out_specs=P(("groups", "ctx"), "head", None),
        check_vma=False,
    )
```

time: 32.1 us -> 27.3 us (0.85)
  Pallas kernels: 30.3 us -> 25.5 us
    pallas_call x1, Pallas kernels: 30.3 us -> 25.5 us  [shards(): call(lengths, queries, prefix_keys.reshape(positions * kv, width), prefix...]
where the time goes in v2:
time: 27.3 us; the launch traced here: 27.2 us
  Pallas kernels  25.5 us (93%)
  local copies, waits for them, and re-layouts  1.62 us (6%)
    pallas_call x1, Pallas kernels, shards(): call(lengths, queries, prefix_keys.reshape(positions * kv, width), prefix...  25.5 us
    unnamed x1, local copies, waits for them, and re-layouts  1.62 us

profile of v2, /device:TPU:0, one launch (start us, length us, event | category | flops | bytes accessed | tf_op | source)
XLA Modules:
  0.0 27.2 jit_solution(6083188768226553832)
XLA Ops:
  0.0 25.5 %shard_map.64 = bf16[48,16,128]{2,1,0:T(8,128)(2,1)} custom-call(s32[48]{0:T(128)} %len_ref.1, bf16[48,16,128]{2,1,0:T(8,128)(2,1)} %q_hbm.1, bf16[4096,128]{1,0:T(8,128)(2,1)} %bitcast.6, bf16[4096,128]{1,0:T(8,128)(2,1)} %bitcast.7, bf16[48,1024,128]{2,1,0:T(8,128)(2,1)} %bitcast.4, bf16[48,1024,128]{2,1,0:T(8,128)(2,1)} %bitcast.5), custom_call_target="tpu_custom_call" | custom-call | tf_op jit(solution)/shard_map/pallas_call | solution.py:405
  25.5 1.6 %copy.8 = bf16[48,16,128]{2,1,0:T(8,128)(2,1)} copy(bf16[48,16,128]{2,1,0:T(8,128)(2,1)} %shard_map.64) | data formatting | bytes 393216

commit v3 on v2

--- a/solution.py
+++ b/solution.py
@@ -19,11 +19,11 @@
 
 
 def kernel(
-    n_ctx, tile_rows, first_tiles,
+    n_ctx, tile_rows,
     len_ref, q_hbm, pk_hbm, pv_hbm, sk_hbm, sv_hbm, out_ref,
     q_raw, qk, k_raw, v_raw, k_cut, v_turn, wide, sk, sv,
     scores_a, scores_b, weights_a, weights_b, top_a, top_b,
-    acc_all, top_all, part, got, suf_acc, suf_top, suf_sum,
+    ask_a, ask_b, near_a, near_b, far_a, far_b, acc_all, top_all, part, got, q_turn, suf_acc, suf_top, suf_sum,
     q_sem, kv_sem, suf_sem, q_send, q_recv, kv_send, kv_recv, p_send, p_recv,
 ):
     rows, heads, width = q_hbm.shape
@@ -71,20 +71,16 @@
     backs = [device(lax.rem(chip - t + chips, chips), core) for t in range(1, chips)]
     twin = device(chip, pair - 1 - core)
     greeted = partners + ([twin] if pair == 2 else [])
-    if greeted:
-        barrier = pltpu.get_barrier_semaphore()
-        for target in greeted:
-            pl.semaphore_signal(
-                barrier, inc=1, device_id=target, device_id_type=pl.DeviceIdType.MESH
-            )
-        pl.semaphore_wait(barrier, len(greeted))
+    barrier = pltpu.get_barrier_semaphore() if greeted else None
+    for target in greeted:
+        pl.semaphore_signal(
+            barrier, inc=1, device_id=target, device_id_type=pl.DeviceIdType.MESH
+        )
 
     q_sends = [
         remote(q_hbm, q_raw.at[t + 1], q_send.at[t], q_recv.at[t], partners[t])
         for t in range(chips - 1)
     ]
-    for copy in q_sends:
-        copy.start()
 
     def start_tile(tile, carry):
         for copy in suffix_copies(tile):
@@ -193,62 +189,93 @@
         return remote(part.at[t, k], got.at[t, k], p_send.at[t, k], p_recv.at[t, k], backs[t])
 
     def run_units(steps):
-        steps = list(steps)
-        for i, (before, unit, after) in enumerate(steps):
+        counts = {unit_scores: 0, suffix_scores: 0}
+        ready_steps = []
+        for before, first, second, unit, after in steps:
+            ready_steps.append((before, first, second, unit, counts[first] % 2, after))
+            counts[first] += 1
+        for i, (before, first, second, unit, at, after) in enumerate(ready_steps):
             if i == 0:
                 before()
-                unit_scores(unit, 0)
-            if i + 1 < len(steps):
-                steps[i + 1][0]()
-                unit_scores(steps[i + 1][1], (i + 1) % 2)
-            unit_sums(unit, i % 2)
+                first(unit, at)
+            if i + 1 < len(ready_steps):
+                before_next, first_next, _, unit_next, at_next, _ = ready_steps[i + 1]
+                before_next()
+                first_next(unit_next, at_next)
+            second(unit, at)
             after()
 
     def nop():
         pass
 
-    column = lax.broadcasted_iota(jnp.int32, (heads, slots), 1)
-    same_head = column % kv == lax.broadcasted_iota(jnp.int32, (heads, slots), 0) // group
-    nothing = jnp.zeros((heads, width), BF16)
-
-    def suffix_pair(r):
-        ask = jnp.concatenate(
-            [
-                jnp.concatenate([q_raw[0, r], nothing], axis=1),
-                jnp.concatenate([nothing, q_raw[0, r + 1]], axis=1),
-            ],
-            axis=0,
-        )
-        both = dot_t(ask, jnp.concatenate([sk[r], sk[r + 1]], axis=1))
-        done = []
-        for i in range(2):
-            live = same_head & (column < len_ref[r + i] * kv)
-            scores = jnp.where(live, both[i * heads : (i + 1) * heads], MASKED)
-            top = jnp.max(scores, axis=1, keepdims=True)
-            weights = jnp.exp2((scores - top) * factor).astype(BF16)
-            total = jnp.sum(weights.astype(F32), axis=1, keepdims=True)
-            done.append((top * factor, weights, total))
-        joined = jnp.concatenate([x[1] for x in done], axis=0)
-        out = jnp.dot(
-            joined, jnp.concatenate([sv[r], sv[r + 1]], axis=1), preferred_element_type=F32
-        )
-        for i in range(2):
-            acc = out[i * heads : (i + 1) * heads, i * width : (i + 1) * width]
-            top = jnp.broadcast_to(done[i][0], (heads, width))
-            total = jnp.broadcast_to(done[i][2], (heads, width))
-            to = pl.ds(pl.multiple_of((r + i) * group, group), group)
-            for k in range(kv):
-                part = slice(k * group, (k + 1) * group)
-                suf_acc[k, to, :] = acc[part]
-                suf_top[k, to, :] = top[part]
-                suf_sum[k, to, :] = total[part]
-
-    def suffix_tile(tile, carry):
+    asks, nears, fars = (ask_a, ask_b), (near_a, near_b), (far_a, far_b)
+    half = slots // 2
+    lane = lax.broadcasted_iota(jnp.int32, (8, LANES), 1)
+    sublane = lax.broadcasted_iota(jnp.int32, (8, LANES), 0)
+    same_head = sublane % kv == lane % heads // group
+    diagonal = lax.broadcasted_iota(jnp.int32, (LANES, LANES), 0) == lax.broadcasted_iota(
+        jnp.int32, (LANES, LANES), 1
+    )
+
+    def upright(row):
+        wide_row = jnp.broadcast_to(row, (LANES, LANES))
+        return jnp.sum(jnp.where(diagonal, wide_row, 0.0), axis=1, keepdims=True)
+
+    def turn_queries():
+        turned = jnp.transpose(q_raw[0].astype(F32).reshape(rows * heads, width)).astype(BF16)
+        for tile in range(tiles):
+            q_turn[tile] = turned[:, tile * LANES : (tile + 1) * LANES]
+
+    def suffix_scores(tile, at):
         for copy in suffix_copies(tile):
             copy.wait()
-        for i in range(0, tile_rows, 2):
-            suffix_pair(tile * tile_rows + i)
-        return carry
+        r0 = tile * tile_rows
+        ask, (near, far) = asks[at], (nears[at], fars[at])
+        turned = q_turn[tile]
+        row_of = lax.broadcasted_iota(jnp.int32, (width, LANES), 1) // heads
+        limit = jnp.zeros((8, LANES), jnp.int32)
+        for r in range(tile_rows):
+            mine = jnp.where(row_of == r, turned, jnp.zeros_like(turned))
+            ask[2 * r * width : (2 * r + 1) * width, 0:LANES] = mine
+            ask[(2 * r + 1) * width : (2 * r + 2) * width, LANES : 2 * LANES] = mine
+            limit = jnp.where(lane // heads == r, len_ref[r0 + r] * kv, limit)
+        limit = jnp.where(same_head, limit, -1)
+        keys = jnp.concatenate(
+            [sk[r0 + r, i * half : (i + 1) * half] for r in range(tile_rows) for i in range(2)], axis=1
+        )
+        both = jnp.dot(keys, ask[...], preferred_element_type=F32).reshape(half // 8, 8, 2 * LANES)
+        slot = sublane[None] + 8 * lax.broadcasted_iota(jnp.int32, (half // 8, 8, LANES), 0)
+        top = None
+        for i in range(2):
+            x = jnp.where(
+                slot < (limit - i * half)[None], both[:, :, i * LANES : (i + 1) * LANES], MASKED
+            )
+            near[i] = x
+            x = jnp.max(x, axis=0)
+            top = x if top is None else jnp.maximum(top, x)
+        far[...] = jnp.broadcast_to(jnp.max(top, axis=0, keepdims=True), (8, LANES))
+
+    def suffix_sums(tile, at):
+        r0 = tile * tile_rows
+        near, far = nears[at], fars[at]
+        total, parts = None, []
+        for i in range(2):
+            x = jnp.exp2((near[i] - far[...][None]) * factor).reshape(half, LANES).astype(BF16)
+            y = jnp.sum(x.astype(F32).reshape(half // 8, 8, LANES), axis=0)
+            total = y if total is None else total + y
+            parts.append(jnp.transpose(x))
+        weights = jnp.concatenate(parts, axis=1)
+        total = jnp.sum(total, axis=0, keepdims=True)
+        top = jnp.broadcast_to(upright(far[0:1] * factor), (LANES, width))
+        total = jnp.broadcast_to(upright(total), (LANES, width))
+        for r in range(tile_rows):
+            acc = jnp.dot(weights[r * heads : (r + 1) * heads], sv[r0 + r], preferred_element_type=F32)
+            to = slice((r0 + r) * group, (r0 + r + 1) * group)
+            for k in range(kv):
+                here = slice(r * heads + k * group, r * heads + (k + 1) * group)
+                suf_acc[k, to, :] = acc[k * group : (k + 1) * group]
+                suf_top[k, to, :] = top[here]
+                suf_sum[k, to, :] = total[here]
 
     all_tiles = chips * flat // columns
     near = flat // columns
@@ -257,14 +284,21 @@
     split_queries(0)
     kv_copies[0].wait()
     split_keys()
+    if greeted:
+        pl.semaphore_wait(barrier, len(greeted))
+    for copy in q_sends:
+        copy.start()
     kv_copies[1].wait()
     turn_values()
     for k in range(kv):
         for copy in kv_sends(k):
             copy.start()
-    run_units([(nop, (0, k, tile), nop) for tile in range(near) for k in range(kv)])
-    lax.fori_loop(0, first_tiles, suffix_tile, 0)
-
+    turn_queries()
+    for ask in asks:
+        ask[...] = jnp.zeros(ask.shape, BF16)
+
+    near_tiles = flat // columns
+    all_tiles = chips * flat // columns
     waited = set()
 
     def ready(block, k, tile):
@@ -292,23 +326,35 @@
 
         return go
 
-    order = [
-        (block, k, tile) for k in range(kv) for tile in range(near, all_tiles) for block in range(blocks)
-    ] + [(block, k, tile) for k in range(kv) for tile in range(near) for block in range(1, blocks)]
-    run_units([(ready(*unit), unit, finish(*unit)) for unit in order])
-    lax.fori_loop(first_tiles, tiles, suffix_tile, 0)
+    def documents(order):
+        return [
+            (ready(*unit), unit_scores, unit_sums, unit, finish(*unit)) for unit in order
+        ]
+
+    def suffixes(tiles_of):
+        return [(nop, suffix_scores, suffix_sums, tile, nop) for tile in tiles_of]
+
+    cut_at = tiles // 2
+    run_units(
+        documents([(0, k, tile) for tile in range(near_tiles) for k in range(kv)])
+        + suffixes(range(cut_at))
+        + documents(
+            [
+                (block, k, tile)
+                for k in range(kv)
+                for tile in range(near_tiles, all_tiles)
+                for block in range(blocks)
+            ]
+        )
+        + documents(
+            [(block, k, tile) for k in range(kv) for tile in range(near_tiles) for block in range(1, blocks)]
+        )
+        + suffixes(range(cut_at, tiles))
+    )
 
     for k in range(kv):
         for t in range(chips - 1):
             partial_copy(t, k).wait_recv()
-    diagonal = lax.broadcasted_iota(jnp.int32, (LANES, LANES), 0) == lax.broadcasted_iota(
-        jnp.int32, (LANES, LANES), 1
-    )
-
-    def upright(row):
-        wide_row = jnp.broadcast_to(row, (LANES, LANES))
-        return jnp.sum(jnp.where(diagonal, wide_row, 0.0), axis=1, keepdims=True)
-
     per = LANES // group
     for c in range(flat // LANES):
         at = slice(c * LANES, (c + 1) * LANES)
@@ -351,9 +397,8 @@
     flat = rows * (heads // kv)
     pair = 2 if n_ctx % 2 == 0 else 1
     others = max(1, n_ctx // pair - 1)
-    tile_rows = math.gcd(rows, 8)
+    tile_rows = LANES // heads
     tiles = rows // tile_rows
-    first_tiles = tiles // 3
     columns = math.gcd(n_ctx // pair * flat, 256)
     tall = width + 16
     piece = math.gcd(positions * kv, 1024)
@@ -361,7 +406,7 @@
     vmem = pltpu.VMEM
     dma = pltpu.SemaphoreType.DMA
     call = pl.pallas_call(
-        functools.partial(kernel, n_ctx, tile_rows, first_tiles),
+        functools.partial(kernel, n_ctx, tile_rows),
         out_shape=jax.ShapeDtypeStruct((rows, heads, width), BF16),
         in_specs=[pl.BlockSpec(memory_space=pltpu.SMEM)] + [anywhere] * 5,
         out_specs=pl.BlockSpec(memory_space=vmem),
@@ -381,11 +426,18 @@
             vmem((positions, columns), BF16),
             vmem((8, columns), F32),
             vmem((8, columns), F32),
+            vmem((2 * tile_rows * width, 2 * LANES), BF16),
+            vmem((2 * tile_rows * width, 2 * LANES), BF16),
+            vmem((2, slots // 16, 8, LANES), F32),
+            vmem((2, slots // 16, 8, LANES), F32),
+            vmem((8, LANES), F32),
+            vmem((8, LANES), F32),
             vmem((kv, tall, n_ctx // pair * flat), F32),
             vmem((kv, 8, n_ctx // pair * flat), F32),
             vmem((others, kv, width + 8, flat), F32),
             vmem((others, kv, width + 8, flat), F32),
         ]
+        + [vmem((tiles, width, LANES), BF16)]
         + [vmem((kv, flat, width), F32)] * 3
         + [
             dma,

time: 27.3 us -> 27.2 us (level)
  no operation moved by 1% of the time
where the time goes in v3:
time: 27.2 us; the launch traced here: 27.1 us
  Pallas kernels  25.4 us (93%)
  local copies, waits for them, and re-layouts  1.62 us (6%)
    pallas_call x1, Pallas kernels, shards(): call(lengths, queries, prefix_keys.reshape(positions * kv, width), prefix...  25.4 us
    unnamed x1, local copies, waits for them, and re-layouts  1.62 us

profile of v3, /device:TPU:0, one launch (start us, length us, event | category | flops | bytes accessed | tf_op | source)
XLA Modules:
  0.0 27.1 jit_solution(15656494883906188190)
XLA Ops:
  0.0 25.4 %shard_map.64 = bf16[48,16,128]{2,1,0:T(8,128)(2,1)} custom-call(s32[48]{0:T(128)} %len_ref.1, bf16[48,16,128]{2,1,0:T(8,128)(2,1)} %q_hbm.1, bf16[4096,128]{1,0:T(8,128)(2,1)} %bitcast.6, bf16[4096,128]{1,0:T(8,128)(2,1)} %bitcast.7, bf16[48,1024,128]{2,1,0:T(8,128)(2,1)} %bitcast.4, bf16[48,1024,128]{2,1,0:T(8,128)(2,1)} %bitcast.5), custom_call_target="tpu_custom_call" | custom-call | tf_op jit(solution)/shard_map/pallas_call | solution.py:457
  25.4 1.6 %copy.8 = bf16[48,16,128]{2,1,0:T(8,128)(2,1)} copy(bf16[48,16,128]{2,1,0:T(8,128)(2,1)} %shard_map.64) | data formatting | bytes 393216

commit v4 on v3

--- a/solution.py
+++ b/solution.py
@@ -12,6 +12,7 @@
 BF16 = jnp.bfloat16
 MASKED = -1e30
 LANES = 128
+CODES = 32767.0
 
 
 def dot_t(a, b):
@@ -23,7 +24,7 @@
     len_ref, q_hbm, pk_hbm, pv_hbm, sk_hbm, sv_hbm, out_ref,
     q_raw, qk, k_raw, v_raw, k_cut, v_turn, wide, sk, sv,
     scores_a, scores_b, weights_a, weights_b, top_a, top_b,
-    ask_a, ask_b, near_a, near_b, far_a, far_b, acc_all, top_all, part, got, q_turn, suf_acc, suf_top, suf_sum,
+    ask_a, ask_b, near_a, near_b, far_a, far_b, acc_all, top_all, part, got, part_stat, got_stat, q_turn, suf_acc, suf_top, suf_sum,
     q_sem, kv_sem, suf_sem, q_send, q_recv, kv_send, kv_recv, p_send, p_recv,
 ):
     rows, heads, width = q_hbm.shape
@@ -77,8 +78,14 @@
             barrier, inc=1, device_id=target, device_id_type=pl.DeviceIdType.MESH
         )
 
+    row_pieces = [(0, rows)]
     q_sends = [
-        remote(q_hbm, q_raw.at[t + 1], q_send.at[t], q_recv.at[t], partners[t])
+        [
+            remote(
+                q_hbm.at[lo:hi], q_raw.at[t + 1, lo:hi], q_send.at[t, i], q_recv.at[t, i], partners[t]
+            )
+            for i, (lo, hi) in enumerate(row_pieces)
+        ]
         for t in range(chips - 1)
     ]
 
@@ -89,10 +96,12 @@
 
     lax.fori_loop(0, tiles, start_tile, 0)
 
-    def split_queries(slot):
-        wide_q = q_raw[slot].astype(F32).reshape(rows, kv, group, width)
+    def split_queries(slot, lo, hi):
+        wide_q = q_raw[slot, lo:hi].astype(F32).reshape(hi - lo, kv, group, width)
         for k in range(kv):
-            qk[k, slot * flat : (slot + 1) * flat] = wide_q[:, k].reshape(flat, width).astype(BF16)
+            qk[k, slot * flat + lo * group : slot * flat + hi * group] = (
+                wide_q[:, k].reshape((hi - lo) * group, width).astype(BF16)
+            )
 
     piece = wide.shape[1]
     cut = piece // kv
@@ -170,7 +179,7 @@
             acc_all[k, :, to] = out
             top_all[k, :, to] = top
             return
-        first = lax.broadcasted_iota(jnp.int32, (8, LANES), 0) == 0
+        row = lax.broadcasted_iota(jnp.int32, (8, LANES), 0)
         for c in range(columns // LANES):
             at_c = tile * columns + c * LANES
             here = slice(c * LANES, (c + 1) * LANES)
@@ -180,13 +189,22 @@
                 top_all[k, :, at_c : at_c + LANES] = top[:, here]
             else:
                 into = slice(within, within + LANES)
-                part[slot - 1, k, 0:width, into] = out[0:width, here]
-                part[slot - 1, k, width : width + 8, into] = jnp.where(
-                    first, out[width : width + 8, here], top[:, here]
-                )
-
-    def partial_copy(t, k):
-        return remote(part.at[t, k], got.at[t, k], p_send.at[t, k], p_recv.at[t, k], backs[t])
+                x = out[0:width, here]
+                most = jnp.max(jnp.max(jnp.abs(x).reshape(width // 8, 8, LANES), axis=0), axis=0, keepdims=True)
+                most = jnp.maximum(most, 1e-33)
+                code = jnp.round(x * (CODES / most)).astype(jnp.int32)
+                part[slot - 1, k, :, into] = code.astype(jnp.int16)
+                stat = jnp.where(row == 1, top[:, here], most * (1.0 / CODES))
+                part_stat[slot - 1, k, :, into] = jnp.where(row == 0, out[width : width + 8, here], stat)
+
+    def partial_copies(t, k, i):
+        at = slice(row_pieces[i][0] * group, row_pieces[i][1] * group)
+        return [
+            remote(
+                src.at[t, k, :, at], dst.at[t, k, :, at], p_send.at[t, k, i, j], p_recv.at[t, k, i, j], backs[t]
+            )
+            for j, (src, dst) in enumerate(((part, got), (part_stat, got_stat)))
+        ]
 
     def run_units(steps):
         counts = {unit_scores: 0, suffix_scores: 0}
@@ -198,6 +216,7 @@
             if i == 0:
                 before()
                 first(unit, at)
+                settle()
             if i + 1 < len(ready_steps):
                 before_next, first_next, _, unit_next, at_next, _ = ready_steps[i + 1]
                 before_next()
@@ -227,8 +246,6 @@
             q_turn[tile] = turned[:, tile * LANES : (tile + 1) * LANES]
 
     def suffix_scores(tile, at):
-        for copy in suffix_copies(tile):
-            copy.wait()
         r0 = tile * tile_rows
         ask, (near, far) = asks[at], (nears[at], fars[at])
         turned = q_turn[tile]
@@ -280,22 +297,31 @@
     all_tiles = chips * flat // columns
     near = flat // columns
 
+    def send_queries():
+        if greeted:
+            pl.semaphore_wait(barrier, len(greeted))
+        for i in range(len(row_pieces)):
+            for t in range(chips - 1):
+                q_sends[t][i].start()
+        for k in range(kv):
+            for copy in kv_sends(k)[:1]:
+                copy.start()
+
+    def settle():
+        kv_copies[1].wait()
+        turn_values()
+        for k in range(kv):
+            for copy in kv_sends(k)[1:]:
+                copy.start()
+        turn_queries()
+        for ask in asks:
+            ask[...] = jnp.zeros(ask.shape, BF16)
+
     q_copy.wait()
-    split_queries(0)
+    split_queries(0, 0, rows)
     kv_copies[0].wait()
     split_keys()
-    if greeted:
-        pl.semaphore_wait(barrier, len(greeted))
-    for copy in q_sends:
-        copy.start()
-    kv_copies[1].wait()
-    turn_values()
-    for k in range(kv):
-        for copy in kv_sends(k):
-            copy.start()
-    turn_queries()
-    for ask in asks:
-        ask[...] = jnp.zeros(ask.shape, BF16)
+    send_queries()
 
     near_tiles = flat // columns
     all_tiles = chips * flat // columns
@@ -303,26 +329,36 @@
 
     def ready(block, k, tile):
         def go():
-            last = ((tile + 1) * columns - 1) // flat
-            for t in range(last):
-                if ("q", t) not in waited:
-                    waited.add(("q", t))
-                    q_sends[t].wait_recv()
-                    split_queries(t + 1)
-            if block > 0 and ("kv", k) not in waited:
-                waited.add(("kv", k))
-                for copy in kv_sends(k):
-                    copy.wait_recv()
+            for t in range(chips - 1):
+                for i, (lo, hi) in enumerate(row_pieces):
+                    begin = (t + 1) * flat + lo * group
+                    if begin < (tile + 1) * columns and ("q", t, i) not in waited:
+                        waited.add(("q", t, i))
+                        q_sends[t][i].wait_recv()
+                        split_queries(t + 1, lo, hi)
+            if block > 0 and "kv" not in waited:
+                waited.add("kv")
+                for each in range(kv):
+                    for copy in kv_sends(each):
+                        copy.wait_recv()
 
         return go
+
+    finished = set()
 
     def finish(block, k, tile):
         def go():
-            if block == blocks - 1:
-                for t in range(chips - 1):
-                    end = (t + 2) * flat
-                    if tile * columns < end <= (tile + 1) * columns:
-                        partial_copy(t, k).start()
+            if block < blocks - 1:
+                return
+            finished.update((k, at) for at in range(tile * columns, (tile + 1) * columns, LANES))
+            for t in range(chips - 1):
+                for i, (lo, hi) in enumerate(row_pieces):
+                    begin, end = (t + 1) * flat + lo * group, (t + 1) * flat + hi * group
+                    done = all((k, at) in finished for at in range(begin, end, LANES))
+                    if done and ("p", t, k, i) not in waited:
+                        waited.add(("p", t, k, i))
+                        for copy in partial_copies(t, k, i):
+                            copy.start()
 
         return go
 
@@ -331,30 +367,47 @@
             (ready(*unit), unit_scores, unit_sums, unit, finish(*unit)) for unit in order
         ]
 
-    def suffixes(tiles_of):
-        return [(nop, suffix_scores, suffix_sums, tile, nop) for tile in tiles_of]
-
-    cut_at = tiles // 2
+    def arrived(tiles_of):
+        def go():
+            for tile in tiles_of:
+                for copy in suffix_copies(tile):
+                    copy.wait()
+
+        return go
+
+    def suffixes(tiles_of, together=False):
+        steps = []
+        for tile in tiles_of:
+            need = ([tile] if not together else list(tiles_of) if tile == tiles_of[0] else [])
+            steps.append((arrived(need), suffix_scores, suffix_sums, tile, nop))
+        return steps
+
+    own_first = documents([(0, k, tile) for tile in range(near_tiles) for k in range(kv)])
+    own_rest = documents(
+        [(block, k, tile) for block in range(1, blocks) for tile in range(near_tiles) for k in range(kv)]
+    )
+    others = documents(
+        [
+            (block, k, tile)
+            for k in range(kv)
+            for tile in range(near_tiles, all_tiles)
+            for block in range(blocks)
+        ]
+    )
+    early = tiles // 3
     run_units(
-        documents([(0, k, tile) for tile in range(near_tiles) for k in range(kv)])
-        + suffixes(range(cut_at))
-        + documents(
-            [
-                (block, k, tile)
-                for k in range(kv)
-                for tile in range(near_tiles, all_tiles)
-                for block in range(blocks)
-            ]
-        )
-        + documents(
-            [(block, k, tile) for k in range(kv) for tile in range(near_tiles) for block in range(1, blocks)]
-        )
-        + suffixes(range(cut_at, tiles))
+        own_first
+        + suffixes(range(early))
+        + own_rest
+        + others
+        + suffixes(range(early, tiles), True)
     )
 
     for k in range(kv):
         for t in range(chips - 1):
-            partial_copy(t, k).wait_recv()
+            for i in range(len(row_pieces)):
+                for copy in partial_copies(t, k, i):
+                    copy.wait_recv()
     per = LANES // group
     for c in range(flat // LANES):
         at = slice(c * LANES, (c + 1) * LANES)
@@ -369,9 +422,9 @@
                 terms = merge(
                     terms,
                     (
-                        got[t, k, width + 1 : width + 2, at],
-                        got[t, k, 0:width, at],
-                        got[t, k, width : width + 1, at],
+                        got_stat[t, k, 1:2, at],
+                        got[t, k, :, at].astype(jnp.int32).astype(F32) * got_stat[t, k, 2:3, at],
+                        got_stat[t, k, 0:1, at],
                     ),
                 )
             terms = merge(
@@ -381,13 +434,16 @@
             done.append((terms[1] / terms[2]).reshape(per, 1, group, width))
         joined = jnp.concatenate(done, axis=1).reshape(per, heads, width)
         out_ref[c * per : (c + 1) * per] = joined.astype(BF16)
-    for copy in q_sends:
-        copy.wait_send()
+    for copies in q_sends:
+        for copy in copies:
+            copy.wait_send()
     for k in range(kv):
         for copy in kv_sends(k):
             copy.wait_send()
         for t in range(chips - 1):
-            partial_copy(t, k).wait_send()
+            for i in range(len(row_pieces)):
+                for copy in partial_copies(t, k, i):
+                    copy.wait_send()
 
 
 def shards(n_ctx, queries, prefix_keys, prefix_values, suffix_keys, suffix_values, lengths):
@@ -434,8 +490,10 @@
             vmem((8, LANES), F32),
             vmem((kv, tall, n_ctx // pair * flat), F32),
             vmem((kv, 8, n_ctx // pair * flat), F32),
-            vmem((others, kv, width + 8, flat), F32),
-            vmem((others, kv, width + 8, flat), F32),
+            vmem((others, kv, width, flat), jnp.int16),
+            vmem((others, kv, width, flat), jnp.int16),
+            vmem((others, kv, 8, flat), F32),
+            vmem((others, kv, 8, flat), F32),
         ]
         + [vmem((tiles, width, LANES), BF16)]
         + [vmem((kv, flat, width), F32)] * 3
@@ -443,12 +501,12 @@
             dma,
             dma((2,)),
             dma((tiles, 2)),
-            dma((others,)),
-            dma((others,)),
+            dma((others, 2)),
+            dma((others, 2)),
             dma((kv, 2)),
             dma((kv, 2)),
-            dma((others, kv)),
-            dma((others, kv)),
+            dma((others, kv, 2, 2)),
+            dma((others, kv, 2, 2)),
         ],
         compiler_params=pltpu.CompilerParams(
             collective_id=0, has_side_effects=True, vmem_limit_bytes=62 * 1024 * 1024

time: 27.2 us -> 24.8 us (0.912)
  Pallas kernels: 25.4 us -> 23 us
    pallas_call x1, Pallas kernels: 25.4 us -> 23 us  [shards(): call(lengths, queries, prefix_keys.reshape(positions * kv, width), prefix...]
where the time goes in v4:
time: 24.8 us; the launch traced here: 24.6 us
  Pallas kernels  23 us (93%)
  local copies, waits for them, and re-layouts  1.62 us (7%)
    pallas_call x1, Pallas kernels, shards(): call(lengths, queries, prefix_keys.reshape(positions * kv, width), prefix...  23 us
    unnamed x1, local copies, waits for them, and re-layouts  1.62 us

profile of v4, /device:TPU:0, one launch (start us, length us, event | category | flops | bytes accessed | tf_op | source)
XLA Modules:
  0.0 24.6 jit_solution(9521795470704013631)
XLA Ops:
  0.0 23.0 %shard_map.64 = bf16[48,16,128]{2,1,0:T(8,128)(2,1)} custom-call(s32[48]{0:T(128)} %len_ref.1, bf16[48,16,128]{2,1,0:T(8,128)(2,1)} %q_hbm.1, bf16[4096,128]{1,0:T(8,128)(2,1)} %bitcast.6, bf16[4096,128]{1,0:T(8,128)(2,1)} %bitcast.7, bf16[48,1024,128]{2,1,0:T(8,128)(2,1)} %bitcast.4, bf16[48,1024,128]{2,1,0:T(8,128)(2,1)} %bitcast.5), custom_call_target="tpu_custom_call" | custom-call | tf_op jit(solution)/shard_map/pallas_call | solution.py:515
  23.0 1.6 %copy.8 = bf16[48,16,128]{2,1,0:T(8,128)(2,1)} copy(bf16[48,16,128]{2,1,0:T(8,128)(2,1)} %shard_map.64) | data formatting | bytes 393216

commit v5 on v4

--- a/solution.py
+++ b/solution.py
@@ -21,11 +21,12 @@
 
 def kernel(
     n_ctx, tile_rows,
-    len_ref, q_hbm, pk_hbm, pv_hbm, sk_hbm, sv_hbm, out_ref,
+    len_hbm, q_hbm, pk_hbm, pv_hbm, sk_hbm, sv_hbm, out_ref,
+    len_ref,
     q_raw, qk, k_raw, v_raw, k_cut, v_turn, wide, sk, sv,
     scores_a, scores_b, weights_a, weights_b, top_a, top_b,
     ask_a, ask_b, near_a, near_b, far_a, far_b, acc_all, top_all, part, got, part_stat, got_stat, q_turn, suf_acc, suf_top, suf_sum,
-    q_sem, kv_sem, suf_sem, q_send, q_recv, kv_send, kv_recv, p_send, p_recv,
+    len_sem, q_sem, kv_sem, suf_sem, q_send, q_recv, kv_send, kv_recv, p_send, p_recv,
 ):
     rows, heads, width = q_hbm.shape
     kv = k_cut.shape[1]
@@ -60,6 +61,8 @@
     ]
     for copy in kv_copies:
         copy.start()
+    len_copy = pltpu.make_async_copy(len_hbm, len_ref, len_sem)
+    len_copy.start()
 
     def suffix_copies(tile):
         at = pl.ds(tile * tile_rows, tile_rows)
@@ -206,6 +209,44 @@
             for j, (src, dst) in enumerate(((part, got), (part_stat, got_stat)))
         ]
 
+    split_at = (tiles - 1) * tile_rows * group // LANES
+
+    def finals(lo, hi):
+        per = LANES // group
+        for c in range(lo, hi):
+            at = slice(c * LANES, (c + 1) * LANES)
+            done = []
+            for k in range(kv):
+                terms = (
+                    top_all[k, 0:1, at],
+                    acc_all[k, 0:width, at],
+                    acc_all[k, width : width + 1, at],
+                )
+                for t in range(chips - 1):
+                    terms = merge(
+                        terms,
+                        (
+                            got_stat[t, k, 1:2, at],
+                            got[t, k, :, at].astype(jnp.int32).astype(F32) * got_stat[t, k, 2:3, at],
+                            got_stat[t, k, 0:1, at],
+                        ),
+                    )
+                terms = merge(
+                    (upright(terms[0]), jnp.transpose(terms[1]), upright(terms[2])),
+                    (suf_top[k, at, :], suf_acc[k, at, :], suf_sum[k, at, :]),
+                )
+                done.append((terms[1] / terms[2]).reshape(per, 1, group, width))
+            joined = jnp.concatenate(done, axis=1).reshape(per, heads, width)
+            out_ref[c * per : (c + 1) * per] = joined.astype(BF16)
+
+    def collect():
+        for k in range(kv):
+            for t in range(chips - 1):
+                for i in range(len(row_pieces)):
+                    for copy in partial_copies(t, k, i):
+                        copy.wait_recv()
+        finals(0, split_at)
+
     def run_units(steps):
         counts = {unit_scores: 0, suffix_scores: 0}
         ready_steps = []
@@ -216,11 +257,16 @@
             if i == 0:
                 before()
                 first(unit, at)
-                settle()
+                kv_copies[1].wait()
+                len_copy.wait()
             if i + 1 < len(ready_steps):
                 before_next, first_next, _, unit_next, at_next, _ = ready_steps[i + 1]
                 before_next()
                 first_next(unit_next, at_next)
+            if i == 0:
+                settle()
+            if i + 1 == len(ready_steps):
+                collect()
             second(unit, at)
             after()
 
@@ -308,7 +354,6 @@
                 copy.start()
 
     def settle():
-        kv_copies[1].wait()
         turn_values()
         for k in range(kv):
             for copy in kv_sends(k)[1:]:
@@ -323,6 +368,7 @@
     split_keys()
     send_queries()
 
+    early = tiles // 3
     near_tiles = flat // columns
     all_tiles = chips * flat // columns
     waited = set()
@@ -359,6 +405,8 @@
                         waited.add(("p", t, k, i))
                         for copy in partial_copies(t, k, i):
                             copy.start()
+                        if t == chips - 2:
+                            take_suffixes()
 
         return go
 
@@ -375,12 +423,16 @@
 
         return go
 
-    def suffixes(tiles_of, together=False):
-        steps = []
-        for tile in tiles_of:
-            need = ([tile] if not together else list(tiles_of) if tile == tiles_of[0] else [])
-            steps.append((arrived(need), suffix_scores, suffix_sums, tile, nop))
-        return steps
+    def take_suffixes():
+        if "rest" not in waited:
+            waited.add("rest")
+            arrived(range(early, tiles))()
+
+    def suffixes(tiles_of):
+        return [
+            (arrived([tile]) if tile < early else take_suffixes, suffix_scores, suffix_sums, tile, nop)
+            for tile in tiles_of
+        ]
 
     own_first = documents([(0, k, tile) for tile in range(near_tiles) for k in range(kv)])
     own_rest = documents(
@@ -394,46 +446,15 @@
             for block in range(blocks)
         ]
     )
-    early = tiles // 3
     run_units(
         own_first
         + suffixes(range(early))
         + own_rest
         + others
-        + suffixes(range(early, tiles), True)
-    )
-
-    for k in range(kv):
-        for t in range(chips - 1):
-            for i in range(len(row_pieces)):
-                for copy in partial_copies(t, k, i):
-                    copy.wait_recv()
-    per = LANES // group
-    for c in range(flat // LANES):
-        at = slice(c * LANES, (c + 1) * LANES)
-        done = []
-        for k in range(kv):
-            terms = (
-                top_all[k, 0:1, at],
-                acc_all[k, 0:width, at],
-                acc_all[k, width : width + 1, at],
-            )
-            for t in range(chips - 1):
-                terms = merge(
-                    terms,
-                    (
-                        got_stat[t, k, 1:2, at],
-                        got[t, k, :, at].astype(jnp.int32).astype(F32) * got_stat[t, k, 2:3, at],
-                        got_stat[t, k, 0:1, at],
-                    ),
-                )
-            terms = merge(
-                (upright(terms[0]), jnp.transpose(terms[1]), upright(terms[2])),
-                (suf_top[k, at, :], suf_acc[k, at, :], suf_sum[k, at, :]),
-            )
-            done.append((terms[1] / terms[2]).reshape(per, 1, group, width))
-        joined = jnp.concatenate(done, axis=1).reshape(per, heads, width)
-        out_ref[c * per : (c + 1) * per] = joined.astype(BF16)
+        + suffixes(range(early, tiles))
+    )
+
+    finals(split_at, flat // LANES)
     for copies in q_sends:
         for copy in copies:
             copy.wait_send()
@@ -464,9 +485,10 @@
     call = pl.pallas_call(
         functools.partial(kernel, n_ctx, tile_rows),
         out_shape=jax.ShapeDtypeStruct((rows, heads, width), BF16),
-        in_specs=[pl.BlockSpec(memory_space=pltpu.SMEM)] + [anywhere] * 5,
+        in_specs=[anywhere] * 6,
         out_specs=pl.BlockSpec(memory_space=vmem),
         scratch_shapes=[
+            pltpu.SMEM((rows,), jnp.int32),
             vmem((1 + others, rows, heads, width), BF16),
             vmem((kv, n_ctx // pair * flat, width), BF16),
             vmem((positions * kv, width), BF16),
@@ -499,6 +521,7 @@
         + [vmem((kv, flat, width), F32)] * 3
         + [
             dma,
+            dma,
             dma((2,)),
             dma((tiles, 2)),
             dma((others, 2)),
@@ -509,10 +532,10 @@
             dma((others, kv, 2, 2)),
         ],
         compiler_params=pltpu.CompilerParams(
-            collective_id=0, has_side_effects=True, vmem_limit_bytes=62 * 1024 * 1024
+            collective_id=0, has_side_effects=True, vmem_limit_bytes=52 * 1024 * 1024
         ),
     )
-    return call(
+    operands = (
         lengths,
         queries,
         prefix_keys.reshape(positions * kv, width),
@@ -520,6 +543,7 @@
         suffix_keys.reshape(rows, slots, width),
         suffix_values.reshape(rows, slots, width),
     )
+    return call(*(pltpu.with_memory_space_constraint(x, pltpu.HBM) for x in operands))
 
 
 def solution(mesh):

time: 24.8 us -> 22.2 us (0.90)
  Pallas kernels: 23 us -> 21.4 us
  local copies, waits for them, and re-layouts: 1.62 us -> 0.68 us
    pallas_call x1, Pallas kernels: 23 us -> 21.4 us  [shards(): call(*(pltpu.with_memory_space_constraint(x, pltpu.HBM) for x in operands))]
    unnamed x1, local copies, waits for them, and re-layouts: 1.62 us -> 0.68 us
where the time goes in v5:
time: 22.2 us; the launch traced here: 22.1 us
  Pallas kernels  21.4 us (96%)
  local copies, waits for them, and re-layouts  0.68 us (3%)
    pallas_call x1, Pallas kernels, shards(): call(*(pltpu.with_memory_space_constraint(x, pltpu.HBM) for x in operands))  21.4 us
    unnamed x1, local copies, waits for them, and re-layouts  0.68 us

profile of v5, /device:TPU:0, one launch (start us, length us, event | category | flops | bytes accessed | tf_op | source)
XLA Modules:
  0.0 22.1 jit_solution(17029589734670952751)
XLA Ops:
  0.0 21.4 %shard_map.64 = bf16[48,16,128]{2,1,0:T(8,128)(2,1)S(1)} custom-call(s32[48]{0:T(128)} %len_hbm.1, bf16[48,16,128]{2,1,0:T(8,128)(2,1)} %q_hbm.1, bf16[4096,128]{1,0:T(8,128)(2,1)} %bitcast.6, bf16[4096,128]{1,0:T(8,128)(2,1)} %bitcast.7, bf16[48,1024,128]{2,1,0:T(8,128)(2,1)} %bitcast.4, bf16[48,1024,128]{2,1,0:T(8,128)(2,1)} %bitcast.5), custom_call_target="tpu_custom_call" | custom-call | tf_op jit(solution)/shard_map/pallas_call | solution.py:546
  21.4 0.7 %copy.8 = bf16[48,16,128]{2,1,0:T(8,128)(2,1)} copy(bf16[48,16,128]{2,1,0:T(8,128)(2,1)S(1)} %shard_map.64) | data formatting | bytes 393216

commit v6 on v5

--- a/solution.py
+++ b/solution.py
@@ -23,7 +23,7 @@
     n_ctx, tile_rows,
     len_hbm, q_hbm, pk_hbm, pv_hbm, sk_hbm, sv_hbm, out_ref,
     len_ref,
-    q_raw, qk, k_raw, v_raw, k_cut, v_turn, wide, sk, sv,
+    q_raw, q_far, qk, k_raw, v_raw, k_cut, v_turn, wide, sk, sv,
     scores_a, scores_b, weights_a, weights_b, top_a, top_b,
     ask_a, ask_b, near_a, near_b, far_a, far_b, acc_all, top_all, part, got, part_stat, got_stat, q_turn, suf_acc, suf_top, suf_sum,
     len_sem, q_sem, kv_sem, suf_sem, q_send, q_recv, kv_send, kv_recv, p_send, p_recv,
@@ -53,7 +53,7 @@
             device_id=target, device_id_type=pl.DeviceIdType.MESH,
         )
 
-    q_copy = pltpu.make_async_copy(q_hbm, q_raw.at[0], q_sem)
+    q_copy = pltpu.make_async_copy(q_hbm, q_raw, q_sem)
     q_copy.start()
     kv_copies = [
         pltpu.make_async_copy(pk_hbm, k_raw, kv_sem.at[0]),
@@ -85,9 +85,10 @@
     q_sends = [
         [
             remote(
-                q_hbm.at[lo:hi], q_raw.at[t + 1, lo:hi], q_send.at[t, i], q_recv.at[t, i], partners[t]
+                q_hbm.at[:, k * group : (k + 1) * group], q_far.at[t, k],
+                q_send.at[t, k], q_recv.at[t, k], partners[t],
             )
-            for i, (lo, hi) in enumerate(row_pieces)
+            for k in range(kv)
         ]
         for t in range(chips - 1)
     ]
@@ -99,12 +100,14 @@
 
     lax.fori_loop(0, tiles, start_tile, 0)
 
-    def split_queries(slot, lo, hi):
-        wide_q = q_raw[slot, lo:hi].astype(F32).reshape(hi - lo, kv, group, width)
+    def split_queries():
+        wide_q = q_raw[...].astype(F32).reshape(rows, kv, group, width)
         for k in range(kv):
-            qk[k, slot * flat + lo * group : slot * flat + hi * group] = (
-                wide_q[:, k].reshape((hi - lo) * group, width).astype(BF16)
-            )
+            qk[k, 0:flat] = wide_q[:, k].reshape(flat, width).astype(BF16)
+
+    def join_queries(t, k):
+        far_q = q_far[t, k].astype(F32).reshape(flat, width).astype(BF16)
+        qk[k, (t + 1) * flat : (t + 2) * flat] = far_q
 
     piece = wide.shape[1]
     cut = piece // kv
@@ -287,7 +290,7 @@
         return jnp.sum(jnp.where(diagonal, wide_row, 0.0), axis=1, keepdims=True)
 
     def turn_queries():
-        turned = jnp.transpose(q_raw[0].astype(F32).reshape(rows * heads, width)).astype(BF16)
+        turned = jnp.transpose(q_raw[...].astype(F32).reshape(rows * heads, width)).astype(BF16)
         for tile in range(tiles):
             q_turn[tile] = turned[:, tile * LANES : (tile + 1) * LANES]
 
@@ -346,9 +349,15 @@
     def send_queries():
         if greeted:
             pl.semaphore_wait(barrier, len(greeted))
-        for i in range(len(row_pieces)):
+        for t in range(chips - 1):
+            q_sends[t][0].start()
+
+    def send_more_queries():
+        for k in range(1, kv):
             for t in range(chips - 1):
-                q_sends[t][i].start()
+                q_sends[t][k].start()
+
+    def send_keys():
         for k in range(kv):
             for copy in kv_sends(k)[:1]:
                 copy.start()
@@ -363,10 +372,11 @@
             ask[...] = jnp.zeros(ask.shape, BF16)
 
     q_copy.wait()
-    split_queries(0, 0, rows)
+    split_queries()
+    send_queries()
     kv_copies[0].wait()
     split_keys()
-    send_queries()
+    send_keys()
 
     early = tiles // 3
     near_tiles = flat // columns
@@ -376,12 +386,10 @@
     def ready(block, k, tile):
         def go():
             for t in range(chips - 1):
-                for i, (lo, hi) in enumerate(row_pieces):
-                    begin = (t + 1) * flat + lo * group
-                    if begin < (tile + 1) * columns and ("q", t, i) not in waited:
-                        waited.add(("q", t, i))
-                        q_sends[t][i].wait_recv()
-                        split_queries(t + 1, lo, hi)
+                if (t + 1) * flat < (tile + 1) * columns and ("q", t, k) not in waited:
+                    waited.add(("q", t, k))
+                    q_sends[t][k].wait_recv()
+                    join_queries(t, k)
             if block > 0 and "kv" not in waited:
                 waited.add("kv")
                 for each in range(kv):
@@ -420,6 +428,8 @@
             for tile in tiles_of:
                 for copy in suffix_copies(tile):
                     copy.wait()
+                if tile == 0:
+                    send_more_queries()
 
         return go
 
@@ -449,8 +459,8 @@
     run_units(
         own_first
         + suffixes(range(early))
+        + others
         + own_rest
-        + others
         + suffixes(range(early, tiles))
     )
 
@@ -489,7 +499,8 @@
         out_specs=pl.BlockSpec(memory_space=vmem),
         scratch_shapes=[
             pltpu.SMEM((rows,), jnp.int32),
-            vmem((1 + others, rows, heads, width), BF16),
+            vmem((rows, heads, width), BF16),
+            vmem((others, kv, rows, heads // kv, width), BF16),
             vmem((kv, n_ctx // pair * flat, width), BF16),
             vmem((positions * kv, width), BF16),
             vmem((positions * kv, width), BF16),
@@ -524,8 +535,8 @@
             dma,
             dma((2,)),
             dma((tiles, 2)),
-            dma((others, 2)),
-            dma((others, 2)),
+            dma((others, kv)),
+            dma((others, kv)),
             dma((kv, 2)),
             dma((kv, 2)),
             dma((others, kv, 2, 2)),

time: 22.2 us -> 20.6 us (0.928)
  Pallas kernels: 21.4 us -> 19.8 us
    pallas_call x1, Pallas kernels: 21.4 us -> 19.8 us  [shards(): call(*(pltpu.with_memory_space_constraint(x, pltpu.HBM) for x in operands))]
where the time goes in v6:
time: 20.6 us; the launch traced here: 20.5 us
  Pallas kernels  19.8 us (96%)
  local copies, waits for them, and re-layouts  0.68 us (3%)
    pallas_call x1, Pallas kernels, shards(): call(*(pltpu.with_memory_space_constraint(x, pltpu.HBM) for x in operands))  19.8 us
    unnamed x1, local copies, waits for them, and re-layouts  0.68 us

profile of v6, /device:TPU:0, one launch (start us, length us, event | category | flops | bytes accessed | tf_op | source)
XLA Modules:
  0.0 20.5 jit_solution(11270047182665597546)
XLA Ops:
  0.0 19.8 %shard_map.64 = bf16[48,16,128]{2,1,0:T(8,128)(2,1)S(1)} custom-call(s32[48]{0:T(128)} %len_hbm.1, bf16[48,16,128]{2,1,0:T(8,128)(2,1)} %q_hbm.1, bf16[4096,128]{1,0:T(8,128)(2,1)} %bitcast.6, bf16[4096,128]{1,0:T(8,128)(2,1)} %bitcast.7, bf16[48,1024,128]{2,1,0:T(8,128)(2,1)} %bitcast.4, bf16[48,1024,128]{2,1,0:T(8,128)(2,1)} %bitcast.5), custom_call_target="tpu_custom_call" | custom-call | tf_op jit(solution)/shard_map/pallas_call | solution.py:557
  19.8 0.7 %copy.8 = bf16[48,16,128]{2,1,0:T(8,128)(2,1)} copy(bf16[48,16,128]{2,1,0:T(8,128)(2,1)S(1)} %shard_map.64) | data formatting | bytes 393216

commit v7 on v6

--- a/solution.py
+++ b/solution.py
@@ -371,9 +371,9 @@
         for ask in asks:
             ask[...] = jnp.zeros(ask.shape, BF16)
 
+    send_queries()
     q_copy.wait()
     split_queries()
-    send_queries()
     kv_copies[0].wait()
     split_keys()
     send_keys()

time: 20.6 us -> 20.4 us (level)
    pallas_call x1, Pallas kernels: 19.8 us -> 19.6 us  [shards(): call(*(pltpu.with_memory_space_constraint(x, pltpu.HBM) for x in operands))]
where the time goes in v7:
time: 20.4 us; the launch traced here: 20.3 us
  Pallas kernels  19.6 us (96%)
  local copies, waits for them, and re-layouts  0.68 us (3%)
    pallas_call x1, Pallas kernels, shards(): call(*(pltpu.with_memory_space_constraint(x, pltpu.HBM) for x in operands))  19.6 us
    unnamed x1, local copies, waits for them, and re-layouts  0.68 us

profile of v7, /device:TPU:0, one launch (start us, length us, event | category | flops | bytes accessed | tf_op | source)
XLA Modules:
  0.0 20.3 jit_solution(6058131215055684211)
XLA Ops:
  0.0 19.6 %shard_map.64 = bf16[48,16,128]{2,1,0:T(8,128)(2,1)S(1)} custom-call(s32[48]{0:T(128)} %len_hbm.1, bf16[48,16,128]{2,1,0:T(8,128)(2,1)} %q_hbm.1, bf16[4096,128]{1,0:T(8,128)(2,1)} %bitcast.6, bf16[4096,128]{1,0:T(8,128)(2,1)} %bitcast.7, bf16[48,1024,128]{2,1,0:T(8,128)(2,1)} %bitcast.4, bf16[48,1024,128]{2,1,0:T(8,128)(2,1)} %bitcast.5), custom_call_target="tpu_custom_call" | custom-call | tf_op jit(solution)/shard_map/pallas_call | solution.py:557
  19.6 0.7 %copy.8 = bf16[48,16,128]{2,1,0:T(8,128)(2,1)} copy(bf16[48,16,128]{2,1,0:T(8,128)(2,1)S(1)} %shard_map.64) | data formatting | bytes 393216
